TPU v7x, 32 devices: a whole 2x2x4 slice. The times are simulated.
32 devices in a mesh: cp: 4 (over z), tp: 8 (over y, x, core).
Axes of the slice: x: 2, y: 2, z: 4, core: 2. Of those that a mesh axis runs over, the one named last changes fastest.
Arguments:
- checkpoint: bfloat16 [2048, 8192], P('cp', 'tp'), may hold values from -6 to 6
- norm_gain: float32 [8192], replicated, may hold values from 0.1 to 1.9
- query_weight: bfloat16 [8192, 8192], P(None, 'tp'), may hold values from -4 to 4
- key_weight: bfloat16 [8192, 1024], P(None, 'tp'), may hold values from -1 to 1
- value_weight: bfloat16 [8192, 1024], P(None, 'tp'), may hold values from -0.0625 to 0.0625
- output_weight: bfloat16 [8192, 8192], P('tp'), may hold values from -0.09375 to 0.09375
- block_order: int32 [8], replicated, may hold values from 0 to 7, each once
Outputs:
- projected: bfloat16 [2048, 8192], P('cp', 'tp')
- log_normalizer: float32 [64, 2048], P('tp', 'cp')
Inputs may be any that keep to these rules, and one draw needn't show every extreme that they name: `block_order`: each of 0 to 7 once.
All inputs are finite; a program needn't handle non-finite values.
Results may differ from a plain program's by a relative error of at most 0.019.
Values may be sent and summed in bfloat16 or wider, within the bound.
A program may use at most 128 MiB of HBM per device.

v0:
```python
import math

import jax
import jax.numpy as jnp
from jax import lax
from jax.sharding import PartitionSpec as P

KV_HEADS = 8
HEAD_DIM = 128


rope_base = 500000.0
norm_epsilon = 1e-05
masked_score = -1e30


def partner_2(block, axis, stride):
    count = lax.axis_size(axis)
    route = []
    for low in range(count):
        high = low | 1 << stride
        if high != low and high < count:
            route += [(low, high), (high, low)]
    return lax.ppermute(block, axis, route)


def from_behind(block, axis, distance):
    devices = range(lax.axis_size(axis))
    route = [((i - distance) % len(devices), i) for i in devices]
    return lax.ppermute(block, axis, route)


def turn_pairs(matrix, positions, first_pair):
    pair_count = matrix.shape[-1] // 2
    pair_index = (first_pair + jnp.arange(pair_count, dtype=jnp.int32)).astype(jnp.float32)
    inverse_rates = rope_base ** (-2.0 * pair_index / HEAD_DIM)
    angles = positions.astype(jnp.float32)[:, None] * inverse_rates[None, :]
    cosine = jnp.cos(angles)[:, None, :]
    sine_part = jnp.sin(angles)[:, None, :]
    paired = matrix.reshape(matrix.shape[0], matrix.shape[1], pair_count, 2)
    former = paired[..., 0]
    latter = paired[..., 1]
    turned = jnp.stack(
        [former * cosine - latter * sine_part, former * sine_part + latter * cosine], axis=-1
    )
    return turned.reshape(matrix.shape)


def shards(
    checkpoint, norm_gain, query_weight, key_weight, value_weight, output_weight, block_order
):
    tok_rows = checkpoint.shape[0]
    block_rows = tok_rows // 2
    local_heads = query_weight.shape[1] // HEAD_DIM
    key_columns = key_weight.shape[1]
    context_rank = lax.axis_index("cp")
    tensor_rank = lax.axis_index("tp")
    row_offsets = jnp.arange(block_rows, dtype=jnp.int32)
    own_blocks = lax.dynamic_slice_in_dim(block_order, 2 * context_rank, 2)
    own_positions = (own_blocks[:, None] * block_rows + row_offsets[None, :]).reshape(tok_rows)
    gathered = lax.all_gather(checkpoint, "tp", axis=1, tiled=True)
    widened = gathered.astype(jnp.float32)
    mean_square = jnp.mean(widened * widened, axis=-1, keepdims=True)
    normed = (widened * lax.rsqrt(mean_square + norm_epsilon) * norm_gain).astype(jnp.bfloat16)
    query_features = jnp.dot(normed, query_weight, preferred_element_type=jnp.float32)
    key_features = jnp.dot(normed, key_weight, preferred_element_type=jnp.float32)
    value_features = jnp.dot(normed, value_weight, preferred_element_type=jnp.float32)
    queries = turn_pairs(
        query_features.reshape(tok_rows, local_heads, HEAD_DIM), own_positions, 0
    ).astype(jnp.bfloat16)
    sharing = lax.axis_size("tp") // KV_HEADS
    part_of_head = tensor_rank % sharing
    key_part = turn_pairs(
        key_features.reshape(tok_rows, 1, key_columns),
        own_positions,
        part_of_head * (key_columns // 2),
    )
    key_part = key_part.astype(jnp.bfloat16).reshape(tok_rows, key_columns)
    value_part = value_features.astype(jnp.bfloat16)
    own_pair = jnp.stack([key_part, value_part])
    if sharing == 2:
        partner = partner_2(own_pair, "tp", 0)
        lower_first = jnp.concatenate([own_pair, partner], axis=-1)
        upper_first = jnp.concatenate([partner, own_pair], axis=-1)
        key_value = jnp.where(part_of_head == 0, lower_first, upper_first)
    else:
        key_value = own_pair
    score_scale = 1.0 / math.sqrt(HEAD_DIM)

    def absorb(running, query_slot, key_block, key_rows, value_rows):
        query_block = own_blocks[query_slot]
        top_scores, totals, weighted = running
        query_rows = queries[query_slot * block_rows : (query_slot + 1) * block_rows]
        scores = (
            jnp.einsum("qhd,kd->qhk", query_rows, key_rows, preferred_element_type=jnp.float32)
            * score_scale
        )
        query_places = query_block * block_rows + row_offsets
        key_places = key_block * block_rows + row_offsets
        allowed = (key_places[None, :] <= query_places[:, None])[:, None, :]
        scores = jnp.where(allowed, scores, masked_score)
        old_top = top_scores[query_slot]
        new_top = jnp.maximum(old_top, jnp.max(scores, axis=-1))
        weights = jnp.where(allowed, jnp.exp(scores - new_top[..., None]), 0.0)
        shrink = jnp.exp(old_top - new_top)
        new_total = totals[query_slot] * shrink + jnp.sum(weights, axis=-1)
        new_sum = weighted[query_slot] * shrink[..., None] + jnp.einsum(
            "qhk,kd->qhd",
            weights.astype(jnp.bfloat16),
            value_rows,
            preferred_element_type=jnp.float32,
        )
        return (
            top_scores.at[query_slot].set(new_top),
            totals.at[query_slot].set(new_total),
            weighted.at[query_slot].set(new_sum),
        )

    def visit_rows(running, key_value_rows, first_row):
        block_count = key_value_rows.shape[1] // block_rows

        def one_block(block_index, current):
            rows_here = lax.dynamic_slice_in_dim(
                key_value_rows, block_index * block_rows, block_rows, 1
            )
            stored = first_row // block_rows + block_index
            key_block = lax.dynamic_index_in_dim(block_order, stored, 0, keepdims=False)
            for query_slot in range(2):
                current = absorb(current, query_slot, key_block, rows_here[0], rows_here[1])
            return current

        return lax.fori_loop(0, block_count, one_block, running)

    running = (
        jnp.full((2, block_rows, local_heads), masked_score, jnp.float32),
        jnp.zeros((2, block_rows, local_heads), jnp.float32),
        jnp.zeros((2, block_rows, local_heads, HEAD_DIM), jnp.float32),
    )
    running = visit_rows(running, key_value, context_rank * tok_rows)
    context_size = lax.axis_size("cp")

    def pass_turn(turn_index, carried):
        current, travelling = carried
        travelling = from_behind(travelling, "cp", 1)
        source = (context_rank - turn_index) % context_size
        return (visit_rows(current, travelling, source * tok_rows), travelling)

    running, unused = lax.fori_loop(1, context_size, pass_turn, (running, key_value))
    top_scores, totals, weighted = running
    attended = (
        (weighted / totals[..., None])
        .astype(jnp.bfloat16)
        .reshape(tok_rows, local_heads * HEAD_DIM)
    )
    normalizer = jnp.transpose((top_scores + jnp.log(totals)).reshape(tok_rows, local_heads))
    partial_terms = jnp.dot(attended, output_weight, preferred_element_type=jnp.float32)
    projected = lax.psum_scatter(
        partial_terms.astype(jnp.bfloat16), "tp", scatter_dimension=1, tiled=True
    )
    return (projected, normalizer)


def solution(mesh):
    return jax.shard_map(
        shards,
        mesh=mesh,
        in_specs=(
            P("cp", "tp"),
            P(),
            P(None, "tp"),
            P(None, "tp"),
            P(None, "tp"),
            P("tp", None),
            P(),
        ),
        out_specs=(P("cp", "tp"), P("tp", "cp")),
        check_vma=False,
    )
```

profile of v0, /device:TPU:0, one launch (start us, length us, event | category | flops | bytes accessed | tf_op | source)
XLA Modules:
  0.0 284.2 jit_solution(17932145199853954866)
XLA Ops:
  11.1 55.8 %all-gather.2.cloned.1.call-done = bf16[512,8192]{1,0:T(8,128)(2,1)} async-done(((bf16[512,1024]{1,0:T(8,128)(2,1)}), bf16[512,8192]{1,0:T(8,128)(2,1)}) %all-gather.2.cloned.1.call-update) | async-done | bytes 8388624 | tf_op jit(solution)/shard_map/all_gather | solution.py:61
  66.9 5.1 %fusion.92 = f32[512]{0:T(512)S(1)} fusion(bf16[512,8192]{1,0:T(8,128)(2,1)} %all-gather.2.cloned.1.call-done), kind=kLoop, calls=%fused_computation.134 | loop fusion | flops 12582400 | bytes 8390656 | tf_op jit(solution)/shard_map/reduce_sum | solution.py:63
  72.0 15.5 %fusion.106 = f32[512,1024]{0,1:T(8,128)} fusion(bf16[8192,1024]{1,0:T(8,128)(2,1)} %param.39, bf16[512,8192]{1,0:T(8,128)(2,1)} %all-gather.2.cloned.1.call-done, f32[8192]{0:T(1024)S(1)} %copy-done.5, f32[512]{0:T(512)S(1)} %add_rsqrt_fusion), kind=kOutput, calls=%fused_computation.165 | convolution fusion | flops 8606711808 | bytes 27297792 | tf_op jit(solution)/shard_map/dot_general | solution.py:65
  87.6 3.5 %reshape_reshape.7 = f32[512,8,64,2]{0,3,2,1:T(2,128)} reshape(f32[512,1024]{0,1:T(8,128)} %fusion.106) | data formatting | bytes 4194304 | tf_op jit(solution)/shard_map/reshape;reshape | solution.py:40
  91.0 5.8 %fusion.109 = f32[512,128]{0,1:T(8,128)S(1)} fusion(bf16[8192,128]{1,0:T(8,128)(2,1)S(1)} %copy-done, bf16[512,8192]{1,0:T(8,128)(2,1)} %all-gather.2.cloned.1.call-done, f32[8192]{0:T(1024)S(1)} %copy-done.5, f32[512]{0:T(512)S(1)} %add_rsqrt_fusion), kind=kOutput, calls=%fused_computation.166 | convolution fusion | flops 1090519040 | bytes 10782720 | tf_op jit(solution)/shard_map/dot_general | solution.py:66
  98.4 2.9 %subtract_convert_fusion = (bf16[512,8,64,1]{0,3,2,1:T(2,128)(2,1)S(1)}, bf16[512,8,64,1]{0,3,2,1:T(2,128)(2,1)S(1)}) fusion(f32[512,8,64,2]{0,3,2,1:T(2,128)S(1)} %copy-done.2, f32[512,64]{0,1:T(8,128)S(1)} %get-tuple-element.1680, f32[512,64]{0,1:T(8,128)S(1)} %get-tuple-element.1679), kind=kLoop, calls=%fused_computation.145 | loop fusion | flops 2097152 | bytes 3407872 | tf_op jit(solution)/shard_map/convert
  101.3 2.2 pad_maximum_fusion
  103.5 1.1 copy.45
  104.7 1.2 copy.46
  105.9 6.4 %fusion.95 = bf16[1,512,128]{2,1,0:T(8,128)(2,1)S(1)} fusion(bf16[8192,128]{1,0:T(8,128)(2,1)} %param.41, bf16[512,8192]{1,0:T(8,128)(2,1)} %all-gather.2.cloned.1.call-done, f32[8192]{0:T(1024)S(1)} %copy-done.5, f32[512]{0:T(512)S(1)} %add_rsqrt_fusion), kind=kOutput, calls=%fused_computation.140 | convolution fusion | flops 1090584576 | bytes 10651648 | tf_op jit(solution)/shard_map/dot_general | solution.py:67
  113.2 11.7 %while.100 = (s32[]{:T(128)}, f32[2,256,8]{1,2,0:T(8,128)S(1)}, f32[2,256,8]{1,2,0:T(8,128)S(1)}, f32[2,256,8,128]{3,1,2,0:T(8,128)S(1)}, s32[]{:T(128)}, /*inde...) while((s32[]{:T(128)}, f32[2,256,8]{1,2,0:T(8,128)S(1)}, ...), condition=%wide.region_6.7_spmd.clone.clone, body=%wide.region_1.6_spmd.clone.clone.sunk | while | flops 551699200 | bytes 24107364 | solution.py:132
  115.9 0.9 fusion.153
  118.1 0.9 fusion.155
  121.7 0.9 fusion.153
  124.0 0.9 fusion.155
  124.9 65.2 %while.102 = (s32[]{:T(128)}, f32[2,256,8]{1,2,0:T(8,128)S(1)}, f32[2,256,8]{1,2,0:T(8,128)S(1)}, f32[2,256,8,128]{3,1,2,0:T(8,128)S(1)}, bf16[2,512,128]{2,1,0:...) while((s32[]{:T(128)}, f32[2,256,8]{1,2,0:T(8,128)S(1)}, ...), condition=%wide.region_14.15_spmd.clone.clone, body=%wide.region_7.14_spmd.clone.clone.sunk | while | flops 551699200 | bytes 24634376 | solution.py:148
  124.9 1.5 collective-permute-start
  126.5 9.0 %collective-permute-done = bf16[2,512,128]{2,1,0:T(8,128)(2,1)S(1)} collective-permute-done((bf16[2,512,128]{2,1,0:T(8,128)(2,1)}, bf16[2,512,128]{2,1,0:T(8,128)(2,1)S(1)}, u32[]{:S(2)}, u32[]{:S(2)}) %collective-permute-start) | collective-permute-done | bytes 262176 | tf_op jit(solution)/shard_map/while/body/eval_jaxpr/ppermute | solution.py:30
  135.5 11.4 %while.103 = (s32[]{:T(128)}, f32[2,256,8]{1,2,0:T(8,128)S(1)}, f32[2,256,8]{1,2,0:T(8,128)S(1)}, f32[2,256,8,128]{3,1,2,0:T(8,128)S(1)}, s32[]{:T(128)}, /*inde...) while((s32[]{:T(128)}, f32[2,256,8]{1,2,0:T(8,128)S(1)}, ...), condition=%wide.region_13.13_spmd.clone, body=%wide.region_8.12_spmd.clone.sunk | while | flops 551699200 | bytes 23059792 | solution.py:132
  140.2 0.9 fusion.168
  145.9 0.9 fusion.168
  147.6 9.6 %collective-permute-done = bf16[2,512,128]{2,1,0:T(8,128)(2,1)S(1)} collective-permute-done((bf16[2,512,128]{2,1,0:T(8,128)(2,1)}, bf16[2,512,128]{2,1,0:T(8,128)(2,1)S(1)}, u32[]{:S(2)}, u32[]{:S(2)}) %collective-permute-start) | collective-permute-done | bytes 262176 | tf_op jit(solution)/shard_map/while/body/eval_jaxpr/ppermute | solution.py:30
  157.2 11.4 %while.103 = (s32[]{:T(128)}, f32[2,256,8]{1,2,0:T(8,128)S(1)}, f32[2,256,8]{1,2,0:T(8,128)S(1)}, f32[2,256,8,128]{3,1,2,0:T(8,128)S(1)}, s32[]{:T(128)}, /*inde...) while((s32[]{:T(128)}, f32[2,256,8]{1,2,0:T(8,128)S(1)}, ...), condition=%wide.region_13.13_spmd.clone, body=%wide.region_8.12_spmd.clone.sunk | while | flops 551699200 | bytes 23059792 | solution.py:132
  161.9 0.9 fusion.168
  167.7 0.9 fusion.168
  169.3 8.7 %collective-permute-done = bf16[2,512,128]{2,1,0:T(8,128)(2,1)S(1)} collective-permute-done((bf16[2,512,128]{2,1,0:T(8,128)(2,1)}, bf16[2,512,128]{2,1,0:T(8,128)(2,1)S(1)}, u32[]{:S(2)}, u32[]{:S(2)}) %collective-permute-start) | collective-permute-done | bytes 262176 | tf_op jit(solution)/shard_map/while/body/eval_jaxpr/ppermute | solution.py:30
  178.0 11.4 %while.103 = (s32[]{:T(128)}, f32[2,256,8]{1,2,0:T(8,128)S(1)}, f32[2,256,8]{1,2,0:T(8,128)S(1)}, f32[2,256,8,128]{3,1,2,0:T(8,128)S(1)}, s32[]{:T(128)}, /*inde...) while((s32[]{:T(128)}, f32[2,256,8]{1,2,0:T(8,128)S(1)}, ...), condition=%wide.region_13.13_spmd.clone, body=%wide.region_8.12_spmd.clone.sunk | while | flops 551699200 | bytes 23059792 | solution.py:132
  182.8 0.9 fusion.168
  188.5 0.9 fusion.168
  190.2 1.0 divide_convert_fusion
  191.8 16.8 %convolution_convert_fusion = bf16[512,8192]{1,0:T(8,128)(2,1)} fusion(bf16[1024,8192]{1,0:T(8,128)(2,1)} %param.42, bf16[64,8,8,128]{3,2,1,0:T(8,128)(2,1)S(1)} %bitcast.277), kind=kOutput, calls=%fused_computation.137 | convolution fusion | flops 8594128896 | bytes 26214400 | tf_op jit(solution)/shard_map/dot_general | solution.py:156
  209.3 68.1 %reduce-scatter.2.cloned.1.call-done = bf16[512,1024]{1,0:T(8,128)(2,1)} async-done(((bf16[512,8192]{1,0:T(8,128)(2,1)}), bf16[512,1024]{1,0:T(8,128)(2,1)}) %reduce-scatter.2.cloned.1.call-update) | async-done | bytes 1048592 | tf_op jit(solution)/shard_map/reduce_scatter | solution.py:157
  (158 shorter events, 39.2 us)
Async XLA Ops:
  7.2 83.9 %copy-start = (bf16[8192,128]{1,0:T(8,128)(2,1)S(1)}, bf16[8192,128]{1,0:T(8,128)(2,1)}, u32[]{:S(2)}) copy-start(bf16[8192,128]{1,0:T(8,128)(2,1)} %param.40) | copy-start | bytes 6291460
  7.2 59.7 %all-gather.2.cloned.1.call-start = ((), (), s32[]{:S(2)}) async-start(), calls=%async_computation.1 | async-start | bytes 9437184 | tf_op jit(solution)/shard_map/all_gather | solution.py:61
  7.9 269.5 %reduce-scatter.2.cloned.1.call-start = ((), (), s32[]{:S(2)}) async-start(), calls=%async_computation.2 | async-start | bytes 9437184 | tf_op jit(solution)/shard_map/reduce_scatter | solution.py:157
  11.1 60.9 %copy-start.5 = (f32[8192]{0:T(1024)S(1)}, f32[8192]{0:T(1024)}, u32[]{:S(2)}) copy-start(f32[8192]{0:T(1024)} %param.38) | copy-start | bytes 98308
  96.8 1.6 copy-start.2
  112.2 0.9 copy-start.4
  113.2 1.6 copy-start.3
  119.1 1.6 copy-start.3
  124.9 10.5 %collective-permute-start = (bf16[2,512,128]{2,1,0:T(8,128)(2,1)}, bf16[2,512,128]{2,1,0:T(8,128)(2,1)S(1)}, u32[]{:S(2)}, u32[]{:S(2)}) collective-permute-start(bf16[2,512,128]{2,1,0:T(8,128)(2,1)} %get-tuple-element.2101), channel_id=1, source_target_pairs={{24,0},{0,8},{8,16},{16,24},{25,1},{1,9},{9,17},{17,25},{26,2},{2,... | collective-permute-start | bytes 786440 | tf_op jit(solution)/shard_map/while/body/eval_jaxpr/ppermute | solution.py:30
  147.6 9.6 %collective-permute-start = (bf16[2,512,128]{2,1,0:T(8,128)(2,1)}, bf16[2,512,128]{2,1,0:T(8,128)(2,1)S(1)}, u32[]{:S(2)}, u32[]{:S(2)}) collective-permute-start(bf16[2,512,128]{2,1,0:T(8,128)(2,1)} %get-tuple-element.2101), channel_id=1, source_target_pairs={{24,0},{0,8},{8,16},{16,24},{25,1},{1,9},{9,17},{17,25},{26,2},{2,... | collective-permute-start | bytes 786440 | tf_op jit(solution)/shard_map/while/body/eval_jaxpr/ppermute | solution.py:30
  169.3 8.7 %collective-permute-start = (bf16[2,512,128]{2,1,0:T(8,128)(2,1)}, bf16[2,512,128]{2,1,0:T(8,128)(2,1)S(1)}, u32[]{:S(2)}, u32[]{:S(2)}) collective-permute-start(bf16[2,512,128]{2,1,0:T(8,128)(2,1)} %get-tuple-element.2101), channel_id=1, source_target_pairs={{24,0},{0,8},{8,16},{16,24},{25,1},{1,9},{9,17},{17,25},{26,2},{2,... | collective-permute-start | bytes 786440 | tf_op jit(solution)/shard_map/while/body/eval_jaxpr/ppermute | solution.py:30
  208.7 68.7 %copy-start.1 = (bf16[8192,128]{1,0:T(8,128)(2,1)S(1)}, bf16[8192,128]{1,0:T(8,128)(2,1)}, u32[]{:S(2)}) copy-start(bf16[8192,128]{1,0:T(8,128)(2,1)} %param.40) | copy-start | bytes 6291460
Sparse Core Ops, SparseCore 0:
  9.9 56.9 all-gather.1
  208.8 68.5 reduce-scatter.1
where the time goes:
time: 285 us; the launch traced here: 284 us
  waiting for transfers between devices  152 us (53%)
  matrix products  66.3 us (23%)
  other arithmetic  26.9 us (9%)
  local copies, waits for them, and re-layouts  15.8 us (6%)
  between operations  15.4 us (5%)
  loops' own time  6.3 us (2%)
    reduce_scatter x1, waiting for transfers between devices, shards(): lax.psum_scatter(partial_terms.astype(jnp.bfloat16), 'tp', scatter_dimens...  68.1 us
    all_gather x1, waiting for transfers between devices, shards(): gathered = lax.all_gather(checkpoint, 'tp', axis=1, tiled=True)  55.8 us
    ppermute x3, waiting for transfers between devices, from_behind(): return lax.ppermute(block, axis, route)  27.3 us
    dot_general x1, matrix products, shards(): jnp.dot(attended, output_weight, preferred_element_type=jnp.float32)  16.8 us
    dot_general x1, matrix products, shards(): jnp.dot(normed, query_weight, preferred_element_type=jnp.float32)  15.5 us
    dot_general x16, matrix products, absorb(): jnp.einsum('qhk,kd->qhd', weights.astype(jnp.bfloat16), value_rows, prefe...  14.3 us
    reduce_sum x16, other arithmetic, absorb(): new_total = totals[query_slot] * shrink + jnp.sum(weights, axis=-1)  8.28 us
    dot_general x16, matrix products, absorb(): jnp.einsum('qhd,kd->qhk', query_rows, key_rows, preferred_element_type=jn...  7.43 us
  transfers between devices with their start and end apart: 5, of which 5 were waited for; matrix products, arithmetic and copies ran while one was open for 1% of the time, Pallas kernels for 0%

commit v1 on v0

v1 whole, which is shorter than its diff:
```python
import functools
import math

import jax
import jax.numpy as jnp
from jax import lax
from jax.experimental import pallas as pl
from jax.experimental.pallas import tpu as pltpu
from jax.sharding import PartitionSpec as P

HEAD_DIM = 128
KV_HEADS = 8
MESH = pl.DeviceIdType.MESH
VMEM_BYTES = 62 * 1024 * 1024

rope_base = 500000.0
norm_epsilon = 1e-05
masked_score = -1e30
LOG2E = 1.4426950408889634


def partner_2(block, axis, stride):
    count = lax.axis_size(axis)
    route = []
    for low in range(count):
        high = low | 1 << stride
        if high != low and high < count:
            route += [(low, high), (high, low)]
    return lax.ppermute(block, axis, route)


def turn_pairs(matrix, positions, first_pair):
    pair_count = matrix.shape[-1] // 2
    pair_index = (first_pair + jnp.arange(pair_count, dtype=jnp.int32)).astype(jnp.float32)
    inverse_rates = rope_base ** (-2.0 * pair_index / HEAD_DIM)
    angles = positions.astype(jnp.float32)[:, None] * inverse_rates[None, :]
    cosine = jnp.cos(angles)[:, None, :]
    sine_part = jnp.sin(angles)[:, None, :]
    paired = matrix.reshape(matrix.shape[0], matrix.shape[1], pair_count, 2)
    former = paired[..., 0]
    latter = paired[..., 1]
    turned = jnp.stack(
        [former * cosine - latter * sine_part, former * sine_part + latter * cosine], axis=-1
    )
    return turned.reshape(matrix.shape)


def project_any(checkpoint, norm_gain, query_weight, key_weight, value_weight, positions):
    rows = checkpoint.shape[0]
    heads = query_weight.shape[1] // HEAD_DIM
    key_columns = key_weight.shape[1]
    gathered = lax.all_gather(checkpoint, "tp", axis=1, tiled=True)
    widened = gathered.astype(jnp.float32)
    mean_square = jnp.mean(widened * widened, axis=-1, keepdims=True)
    normed = (widened * lax.rsqrt(mean_square + norm_epsilon) * norm_gain).astype(jnp.bfloat16)
    query_features = jnp.dot(normed, query_weight, preferred_element_type=jnp.float32)
    key_features = jnp.dot(normed, key_weight, preferred_element_type=jnp.float32)
    value_features = jnp.dot(normed, value_weight, preferred_element_type=jnp.float32)
    turned = turn_pairs(query_features.reshape(rows, heads, HEAD_DIM), positions, 0)
    queries = (turned * (LOG2E / math.sqrt(HEAD_DIM))).astype(jnp.bfloat16)
    sharing = lax.axis_size("tp") // KV_HEADS
    part_of_head = lax.axis_index("tp") % sharing
    key_part = turn_pairs(
        key_features.reshape(rows, 1, key_columns), positions, part_of_head * (key_columns // 2)
    )
    key_part = key_part.astype(jnp.bfloat16).reshape(rows, key_columns)
    own_pair = jnp.stack([key_part, value_features.astype(jnp.bfloat16)])
    key_value = own_pair
    if sharing == 2:
        partner = partner_2(own_pair, "tp", 0)
        lower_first = jnp.concatenate([own_pair, partner], axis=-1)
        upper_first = jnp.concatenate([partner, own_pair], axis=-1)
        key_value = jnp.where(part_of_head == 0, lower_first, upper_first)
    return (
        queries.reshape(rows, heads * HEAD_DIM),
        jnp.concatenate([key_value[0], key_value[1]], axis=-1),
    )


def flipped(me, offset):
    result = me
    for bit in (1, 2, 4):
        if offset & bit:
            result = result + bit - 2 * bit * lax.rem(lax.div(me, bit), 2)
    return result


def greet(axis, others):
    barrier = pltpu.get_barrier_semaphore()
    for other in others:
        pl.semaphore_signal(barrier, inc=1, device_id={axis: other}, device_id_type=MESH)
    pl.semaphore_wait(barrier, len(others))


def sender(axis, send_sems, recv_sems):
    used = []

    def make(source, target, other):
        index = len(used)
        copy = pltpu.make_async_remote_copy(
            src_ref=source,
            dst_ref=target,
            send_sem=send_sems.at[index],
            recv_sem=recv_sems.at[index],
            device_id={axis: other},
            device_id_type=MESH,
        )
        used.append(copy)
        return copy

    return make, used


def project_kernel(
    x_hbm, gain_ref, wq_hbm, wk_hbm, wv_hbm, cos_ref, sin_ref,
    q_ref, kv_ref,
    held, weights, gains, acc, scaled, squares, x_sem, w_sems, send_sems, recv_sems,
):
    me = lax.axis_index("tp")
    rows, depth = x_hbm.shape
    half = rows // 2
    q_cols = wq_hbm.shape[1]
    k_cols = wk_hbm.shape[1]
    sib, nx, ny = flipped(me, 1), flipped(me, 2), flipped(me, 4)
    x_copy = pltpu.make_async_copy(x_hbm, held.at[0], x_sem)
    x_copy.start()
    w_copies = []
    for e in range(8):
        chunk = pl.ds(pl.multiple_of(flipped(me, e) * depth, depth), depth)
        parts = (
            (wq_hbm, 0, q_cols),
            (wk_hbm, q_cols, k_cols),
            (wv_hbm, q_cols + k_cols, k_cols),
        )
        w_copies.append(
            [
                pltpu.make_async_copy(
                    w.at[chunk, :], weights.at[e, :, pl.ds(at, size)], w_sems.at[e, i]
                )
                for i, (w, at, size) in enumerate(parts)
            ]
        )
    for copies in w_copies:
        for copy in copies:
            copy.start()
    greet("tp", (sib, nx, ny))
    x_copy.wait()
    make, used = sender("tp", send_sems, recv_sems)

    def part(slot, h):
        return held.at[slot, pl.ds(h * half, half), :]

    dx = [make(part(0, h), part(2, h), nx) for h in range(2)]
    dy = [make(part(0, h), part(4, h), ny) for h in range(2)]
    d1 = make(held.at[0], held.at[1], sib)
    forward_y = make(part(2, 0), part(6, 0), ny)
    forward_x = make(part(4, 1), part(6, 1), nx)
    d3 = [make(part(2, h), part(3, h), sib) for h in range(2)]
    d5 = [make(part(4, h), part(5, h), sib) for h in range(2)]
    d7 = [make(part(6, h), part(7, h), sib) for h in range(2)]
    dx[0].start()
    dy[1].start()
    dx[1].start()
    dy[0].start()
    d1.start()

    squares[...] = jnp.zeros_like(squares)
    acc[...] = jnp.zeros_like(acc)
    for e in range(8):
        gains[e] = gain_ref[pl.ds(flipped(me, e), 1), :]

    def process(e):
        for copy in w_copies[e]:
            copy.wait()

        @pl.loop(0, rows // 64)
        def _(i):
            at = pl.ds(pl.multiple_of(i * 64, 64), 64)
            wide = held[e, at, :].astype(jnp.float32)
            squares[at, :] += jnp.sum(wide * wide, axis=1, keepdims=True)
            scaled[at, :] = (wide * gains[e]).astype(jnp.bfloat16)

        @pl.loop(0, (q_cols + 2 * k_cols) // 256)
        def _(t):
            at = pl.ds(pl.multiple_of(t * 256, 256), 256)
            acc[:, at] += jnp.dot(
                scaled[...], weights[e, :, at], preferred_element_type=jnp.float32
            )

    process(0)
    d1.wait_recv()
    process(1)
    dx[0].wait_recv()
    forward_y.start()
    d3[0].start()
    dy[1].wait_recv()
    forward_x.start()
    d5[1].start()
    dx[1].wait_recv()
    d3[1].start()
    dy[0].wait_recv()
    d5[0].start()
    process(2)
    process(4)
    d3[0].wait_recv()
    d3[1].wait_recv()
    process(3)
    d5[0].wait_recv()
    d5[1].wait_recv()
    process(5)
    forward_y.wait_recv()
    d7[0].start()
    forward_x.wait_recv()
    d7[1].start()
    process(6)
    d7[0].wait_recv()
    d7[1].wait_recv()
    process(7)

    score_scale = LOG2E / math.sqrt(HEAD_DIM)
    features = depth * 8

    @pl.loop(0, rows // 64)
    def _(i):
        at = pl.ds(pl.multiple_of(i * 64, 64), 64)
        rate = lax.rsqrt(squares[at, :] * (1.0 / features) + norm_epsilon)
        cosine = cos_ref[at, :]
        sine = sin_ref[at, :]
        even = lax.rem(lax.broadcasted_iota(jnp.int32, (64, HEAD_DIM), 1), 2) == 0

        def turned(block):
            later = pltpu.roll(block, HEAD_DIM - 1, 1)
            former = pltpu.roll(block, 1, 1)
            return block * cosine + jnp.where(even, later, former) * sine

        for h in range(q_cols // HEAD_DIM):
            cols = pl.ds(h * HEAD_DIM, HEAD_DIM)
            q_ref[at, cols] = turned(acc[at, cols] * (rate * score_scale)).astype(jnp.bfloat16)
        keys = acc[at, pl.ds(q_cols, k_cols)] * rate
        kv_ref[at, pl.ds(0, k_cols)] = turned(keys).astype(jnp.bfloat16)
        values = acc[at, pl.ds(q_cols + k_cols, k_cols)] * rate
        kv_ref[at, pl.ds(k_cols, k_cols)] = values.astype(jnp.bfloat16)

    for copy in used:
        copy.wait_send()


def attend_kernel(
    n_cp, order_ref, q_ref, kv_hbm, out_ref, norm_ref,
    ring, extended, bias, top, weighted, norms, kv_sem, send_sems, recv_sems,
):
    me = lax.axis_index("cp")
    rows = q_ref.shape[0]
    block = rows // 2
    heads = q_ref.shape[1] // HEAD_DIM
    right, left = lax.rem(me + 1, n_cp), lax.rem(me + n_cp - 1, n_cp)
    own_copy = pltpu.make_async_copy(kv_hbm, ring.at[0], kv_sem)
    own_copy.start()
    greet("cp", (right, left))
    own_copy.wait()

    def hop(step, h):
        at = pl.ds(h * block, block)
        return pltpu.make_async_remote_copy(
            src_ref=ring.at[step, at, :],
            dst_ref=ring.at[step + 1, at, :],
            send_sem=send_sems.at[step, h],
            recv_sem=recv_sems.at[step, h],
            device_id={"cp": right},
            device_id_type=MESH,
        )

    hop(0, 0).start()
    hop(0, 1).start()
    extended[:, HEAD_DIM:] = jnp.ones((rows, HEAD_DIM), jnp.bfloat16)
    top[...] = jnp.full(top.shape, masked_score, jnp.float32)
    weighted[...] = jnp.zeros_like(weighted)

    def visit(step, carried):
        for h in range(2):

            @pl.when(step > 0)
            def _():
                hop(step - 1, h).wait_recv()

            @pl.when(jnp.logical_and(step > 0, step < n_cp - 1))
            def _():
                hop(step, h).start()

        owner = lax.rem(me - step + n_cp, n_cp)
        extended[:, :HEAD_DIM] = ring[step, :, HEAD_DIM:]
        base = lax.broadcasted_iota(jnp.int32, (block, block), 0) - lax.broadcasted_iota(
            jnp.int32, (block, block), 1
        )
        for i in range(2):
            for j in range(2):
                ahead = (order_ref[2 * me + i] - order_ref[2 * owner + j]) * block
                bias[i * block : (i + 1) * block, j * block : (j + 1) * block] = jnp.where(
                    base + ahead >= 0, 0.0, masked_score
                )

        def one_head(h, inner):
            cols = pl.ds(pl.multiple_of(h * HEAD_DIM, HEAD_DIM), HEAD_DIM)
            keys = ring[step, :, :HEAD_DIM]
            for i in range(2):
                at = pl.ds(i * block, block)
                scores = lax.dot_general(
                    q_ref[at, cols], keys, (((1,), (1,)), ((), ())),
                    preferred_element_type=jnp.float32,
                )
                scores = scores + bias[at, :]
                old_top = top[h, at, :]
                new_top = jnp.maximum(old_top, jnp.max(scores, axis=1, keepdims=True))
                weights = jnp.exp2(scores - new_top).astype(jnp.bfloat16)
                shrink = jnp.exp2(old_top - new_top)
                top[h, at, :] = new_top
                weighted[h, at, :] = weighted[h, at, :] * shrink + jnp.dot(
                    weights, extended[...], preferred_element_type=jnp.float32
                )
            return inner

        lax.fori_loop(0, heads, one_head, 0)
        return carried

    lax.fori_loop(0, n_cp, visit, 0)
    lane = lax.broadcasted_iota(jnp.int32, (rows, HEAD_DIM), 1)
    norms[...] = jnp.zeros_like(norms)
    for h in range(heads):
        totals = weighted[h, :, HEAD_DIM:]
        out_ref[:, h * HEAD_DIM : (h + 1) * HEAD_DIM] = (
            weighted[h, :, :HEAD_DIM] / totals
        ).astype(jnp.bfloat16)
        norm = (top[h] + jnp.log2(totals)) * (1.0 / LOG2E)
        norms[...] = jnp.where(lane == h, norm, norms[...])
    norm_ref[...] = jnp.transpose(norms[...])[:heads, :]

    for step in range(n_cp - 1):
        for h in range(2):
            hop(step, h).wait_send()


def output_kernel(
    a_ref, w_hbm, out_ref,
    weights, terms, sums, from_sib, from_six, from_x, from_y, w_sems, send_sems, recv_sems,
):
    me = lax.axis_index("tp")
    rows, depth = a_ref.shape
    cols = out_ref.shape[1]
    half = cols // 2
    sib, nx, ny = flipped(me, 1), flipped(me, 2), flipped(me, 4)
    order = [
        (7, 0), (6, 0), (7, 1), (6, 1), (3, 0), (2, 0), (5, 1), (4, 1),
        (3, 1), (2, 1), (5, 0), (4, 0), (1, 0), (0, 0), (1, 1), (0, 1),
    ]
    w_copies = {}
    for e, h in order:
        at = pl.ds(pl.multiple_of(flipped(me, e) * cols + h * half, half), half)
        w_copies[e, h] = pltpu.make_async_copy(w_hbm.at[:, at], weights.at[e, h], w_sems.at[e, h])
        w_copies[e, h].start()
    greet("tp", (sib, nx, ny))
    make, used = sender("tp", send_sems, recv_sems)
    to_sib = {
        (e, h): make(terms.at[e, h], from_sib.at[e // 2, h], sib) for e in (1, 3, 5, 7) for h in (0, 1)
    }
    six_x = make(sums.at[3, 0], from_six.at[0], nx)
    six_y = make(sums.at[3, 1], from_six.at[1], ny)
    to_x = [make(sums.at[1, h], from_x.at[h], nx) for h in (0, 1)]
    to_y = [make(sums.at[2, h], from_y.at[h], ny) for h in (0, 1)]

    def term(e, h):
        w_copies[e, h].wait()

        @pl.loop(0, half // 256)
        def _(t):
            at = pl.ds(pl.multiple_of(t * 256, 256), 256)
            terms[e, h, :, at] = jnp.dot(
                a_ref[...], weights[e, h, :, at], preferred_element_type=jnp.float32
            ).astype(jnp.bfloat16)

        if e % 2:
            to_sib[e, h].start()

    def summed(e, h, others, target):
        to_sib[e + 1, h].wait_recv()

        @pl.loop(0, rows // 64)
        def _(i):
            at = pl.ds(pl.multiple_of(i * 64, 64), 64)
            total = terms[e, h, at, :].astype(jnp.float32)
            total = total + from_sib[e // 2, h, at, :].astype(jnp.float32)
            for other in others:
                total = total + other[at, :].astype(jnp.float32)
            target[at, :] = total.astype(jnp.bfloat16)

    term(7, 0)
    term(6, 0)
    summed(6, 0, (), sums.at[3, 0])
    six_x.start()
    term(7, 1)
    term(6, 1)
    summed(6, 1, (), sums.at[3, 1])
    six_y.start()
    term(3, 0)
    term(2, 0)
    summed(2, 0, (), sums.at[1, 0])
    to_x[0].start()
    term(5, 1)
    term(4, 1)
    summed(4, 1, (), sums.at[2, 1])
    to_y[1].start()
    term(3, 1)
    term(2, 1)
    term(5, 0)
    term(4, 0)
    six_x.wait_recv()
    summed(4, 0, (from_six.at[0],), sums.at[2, 0])
    to_y[0].start()
    six_y.wait_recv()
    summed(2, 1, (from_six.at[1],), sums.at[1, 1])
    to_x[1].start()
    term(1, 0)
    term(0, 0)
    term(1, 1)
    term(0, 1)
    for h in (0, 1):
        to_x[h].wait_recv()
        to_y[h].wait_recv()
        summed(0, h, (from_x.at[h], from_y.at[h]), out_ref.at[:, pl.ds(h * half, half)])
    for copy in used:
        copy.wait_send()


def shards(
    n_cp, n_tp, checkpoint, norm_gain, query_weight, key_weight, value_weight, output_weight, block_order
):
    rows, depth = checkpoint.shape
    q_cols = query_weight.shape[1]
    k_cols = key_weight.shape[1]
    heads = q_cols // HEAD_DIM
    block = rows // 2
    context_rank = lax.axis_index("cp")
    own_blocks = lax.dynamic_slice_in_dim(block_order, 2 * context_rank, 2)
    offsets = jnp.arange(block, dtype=jnp.int32)
    positions = (own_blocks[:, None] * block + offsets[None, :]).reshape(rows)
    lanes = jnp.arange(HEAD_DIM, dtype=jnp.int32)
    rates = rope_base ** (-2.0 * (lanes // 2).astype(jnp.float32) / HEAD_DIM)
    angles = positions.astype(jnp.float32)[:, None] * rates[None, :]
    cosine = jnp.cos(angles)
    sine = jnp.where(lanes % 2 == 0, -1.0, 1.0)[None, :] * jnp.sin(angles)

    any_spec = pl.BlockSpec(memory_space=pl.ANY)
    vmem = pl.BlockSpec(memory_space=pltpu.VMEM)
    smem = pl.BlockSpec(memory_space=pltpu.SMEM)
    bf16, f32 = jnp.bfloat16, jnp.float32
    dma = pltpu.SemaphoreType.DMA

    if n_tp == 8:
        queries, key_value = pl.pallas_call(
            project_kernel,
            out_shape=(
                jax.ShapeDtypeStruct((rows, q_cols), bf16),
                jax.ShapeDtypeStruct((rows, 2 * k_cols), bf16),
            ),
            in_specs=[any_spec, vmem, any_spec, any_spec, any_spec, vmem, vmem],
            out_specs=(vmem, vmem),
            scratch_shapes=[
                pltpu.VMEM((8, rows, depth), bf16),
                pltpu.VMEM((8, depth, q_cols + 2 * k_cols), bf16),
                pltpu.VMEM((8, 1, depth), f32),
                pltpu.VMEM((rows, q_cols + 2 * k_cols), f32),
                pltpu.VMEM((rows, depth), bf16),
                pltpu.VMEM((rows, 1), f32),
                dma,
                dma((8, 3)),
                dma((13,)),
                dma((13,)),
            ],
            compiler_params=pltpu.CompilerParams(
                collective_id=0, has_side_effects=True, vmem_limit_bytes=VMEM_BYTES
            ),
            name="project",
        )(
            checkpoint, norm_gain.reshape(-1, depth), query_weight, key_weight, value_weight, cosine, sine
        )
    else:
        queries, key_value = project_any(
            checkpoint, norm_gain, query_weight, key_weight, value_weight, positions
        )

    attended, normalizer = pl.pallas_call(
        functools.partial(attend_kernel, n_cp),
        out_shape=(
            jax.ShapeDtypeStruct((rows, q_cols), bf16),
            jax.ShapeDtypeStruct((heads, rows), f32),
        ),
        in_specs=[smem, vmem, any_spec],
        out_specs=(vmem, vmem),
        scratch_shapes=[
            pltpu.VMEM((n_cp, rows, 2 * HEAD_DIM), bf16),
            pltpu.VMEM((rows, 2 * HEAD_DIM), bf16),
            pltpu.VMEM((rows, rows), f32),
            pltpu.VMEM((heads, rows, 1), f32),
            pltpu.VMEM((heads, rows, 2 * HEAD_DIM), f32),
            pltpu.VMEM((rows, HEAD_DIM), f32),
            dma,
            dma((n_cp - 1, 2)),
            dma((n_cp - 1, 2)),
        ],
        compiler_params=pltpu.CompilerParams(
            collective_id=1, has_side_effects=True, vmem_limit_bytes=VMEM_BYTES
        ),
        name="attend",
    )(block_order, queries, key_value)

    if n_tp != 8:
        partial_terms = jnp.dot(attended, output_weight, preferred_element_type=jnp.float32)
        projected = lax.psum_scatter(
            partial_terms.astype(bf16), "tp", scatter_dimension=1, tiled=True
        )
        return (projected, normalizer)

    out_cols = output_weight.shape[1] // n_tp
    half = out_cols // 2
    projected = pl.pallas_call(
        output_kernel,
        out_shape=jax.ShapeDtypeStruct((rows, out_cols), bf16),
        in_specs=[vmem, any_spec],
        out_specs=vmem,
        scratch_shapes=[
            pltpu.VMEM((8, 2, q_cols, half), bf16),
            pltpu.VMEM((8, 2, rows, half), bf16),
            pltpu.VMEM((4, 2, rows, half), bf16),
            pltpu.VMEM((4, 2, rows, half), bf16),
            pltpu.VMEM((2, rows, half), bf16),
            pltpu.VMEM((2, rows, half), bf16),
            pltpu.VMEM((2, rows, half), bf16),
            dma((8, 2)),
            dma((14,)),
            dma((14,)),
        ],
        compiler_params=pltpu.CompilerParams(
            collective_id=2, has_side_effects=True, vmem_limit_bytes=VMEM_BYTES
        ),
        name="project_out",
    )(attended, output_weight)
    return (projected, normalizer)


def solution(mesh):
    return jax.shard_map(
        functools.partial(shards, mesh.shape["cp"], mesh.shape["tp"]),
        mesh=mesh,
        in_specs=(
            P("cp", "tp"),
            P(),
            P(None, "tp"),
            P(None, "tp"),
            P(None, "tp"),
            P("tp", None),
            P(),
        ),
        out_specs=(P("cp", "tp"), P("tp", "cp")),
        check_vma=False,
    )
```

time: 285 us -> 149 us (0.52)
  waiting for transfers between devices: 152 us -> 0 us
  Pallas kernels: 0 us -> 141 us
  matrix products: 66.3 us -> 0 us
  other arithmetic: 26.9 us -> 2.61 us
  between operations: 15.4 us -> 0.67 us
  local copies, waits for them, and re-layouts: 15.8 us -> 4.26 us
  loops' own time: 6.3 us -> 0 us
    pallas_call x0 -> x3, Pallas kernels: none -> 141 us  [the longest x1 58.6 us: shards(): pl.pallas_call(project_kernel, out_shape=(jax.ShapeDtypeStruct((rows, q_c...]
    reduce_scatter x1 -> x0, waiting for transfers between devices: 68.1 us -> none  [shards(): lax.psum_scatter(partial_terms.astype(jnp.bfloat16), 'tp', scatter_dimens...]
    dot_general x36 -> x0, matrix products: 66.3 us -> none  [the longest x1 16.8 us: shards(): jnp.dot(attended, output_weight, preferred_element_type=jnp.float32)]
    all_gather x1 -> x0, waiting for transfers between devices: 55.8 us -> none  [shards(): gathered = lax.all_gather(checkpoint, 'tp', axis=1, tiled=True)]
    ppermute x3 -> x0, waiting for transfers between devices: 27.3 us -> none  [from_behind(): return lax.ppermute(block, axis, route)]
    reduce_sum x17 -> x0, other arithmetic: 13.4 us -> none  [the longest x16 8.28 us: absorb(): new_total = totals[query_slot] * shrink + jnp.sum(weights, axis=-1)]
    another operation x5 -> x0, other arithmetic: 6.39 us -> none
    another operation x5 -> x0, loops' own time: 6.3 us -> none  [the longest x4 6.26 us: visit_rows(): return lax.fori_loop(0, block_count, one_block, running)]
  transfers between devices with their start and end apart: 5 -> 0, of which waited for: 5 -> 0; matrix products, arithmetic and copies ran while one was open for 1% -> 0% of each run, Pallas kernels for 0% -> 0%
where the time goes in v1:
time: 149 us
  Pallas kernels  141 us (95%)
  local copies, waits for them, and re-layouts  4.26 us (3%)
  other arithmetic  2.61 us (2%)
    pallas_call x1, Pallas kernels, shards(): pl.pallas_call(project_kernel, out_shape=(jax.ShapeDtypeStruct((rows, q_c...  58.6 us
    pallas_call x1, Pallas kernels, shards(): pl.pallas_call(output_kernel, out_shape=jax.ShapeDtypeStruct((rows, out_c...  45.4 us
    pallas_call x1, Pallas kernels, shards(): pl.pallas_call(functools.partial(attend_kernel, n_cp), out_shape=(jax.Sha...  37.3 us

profile of v1, /device:TPU:0, one launch (start us, length us, event | category | flops | bytes accessed | tf_op | source)
XLA Modules:
  0.0 148.8 jit_solution(16341442707047140504)
XLA Ops:
  0.6 0.7 dynamic-slice_multiply_fusion
  1.4 0.1 convert_bitcast_fusion
  1.5 1.4 reshape.51.gain_ref
  2.8 1.8 %fusion = (f32[512,128]{1,0:T(8,128)}, f32[512,128]{1,0:T(8,128)}) fusion(f32[128]{0:T(128)S(1)} %get-tuple-element.12, f32[128]{0:T(128)S(1)} %get-tuple-element.13, f32[512]{0:T(512)S(1)} %bitcast.3), kind=kLoop, calls=%fused_computation.2 | loop fusion | flops 131072 | bytes 527360 | tf_op jit(solution)/shard_map/mul | solution.py:449
  4.6 58.6 %project.1 = (bf16[512,1024]{1,0:T(8,128)(2,1)}, bf16[512,256]{1,0:T(8,128)(2,1)}) custom-call(bf16[512,1024]{1,0:T(8,128)(2,1)} %x_hbm.1, f32[8,1024]{1,0:T(8,128)} %reshape.51.gain_ref, bf16[8192,1024]{1,0:T(8,128)(2,1)} %wq_hbm.1, bf16[8192,128]{1,0:T(8,128)(2,1)} %wk_hbm.1, bf16[8192,128]{1,0:T(8,128)(2,1)} %wv_hbm.1, ...), custom_call_target="tpu_custom_call" | custom-call | tf_op jit(solution)/shard_map/project/pallas_call | solution.py:458
  63.3 37.3 %attend.1 = (bf16[512,1024]{1,0:T(8,128)(2,1)}, f32[8,512]{1,0:T(8,128)}) custom-call(s32[8]{0:T(128)} %order_ref.1, bf16[512,1024]{1,0:T(8,128)(2,1)} %get-tuple-element.6.q_ref, bf16[512,256]{1,0:T(8,128)(2,1)} %get-tuple-element.7.kv_hbm), custom_call_target="tpu_custom_call" | custom-call | tf_op jit(solution)/shard_map/attend/pallas_call | solution.py:490
  100.5 0.0 copy-start
  100.5 45.4 %project_out.1 = bf16[512,1024]{1,0:T(8,128)(2,1)} custom-call(bf16[512,1024]{1,0:T(8,128)(2,1)} %get-tuple-element.8.a_ref, bf16[1024,8192]{1,0:T(8,128)(2,1)} %w_hbm.1), custom_call_target="tpu_custom_call" | custom-call | tf_op jit(solution)/shard_map/project_out/pallas_call | solution.py:524
  145.9 2.3 %copy.12 = bf16[512,1024]{1,0:T(8,128)(2,1)} copy(bf16[512,1024]{1,0:T(8,128)(2,1)} %project_out.1) | data formatting | bytes 2097152
  148.2 0.0 copy-done
  148.2 0.6 copy.13
  (2 shorter events, 0.0 us)
Async XLA Ops:
  100.5 47.6 %copy-start = (f32[8,512]{1,0:T(8,128)S(1)}, f32[8,512]{1,0:T(8,128)}, u32[]{:S(2)}) copy-start(f32[8,512]{1,0:T(8,128)} %get-tuple-element.17) | copy-start | bytes 49156

commit v2 on v1

--- a/solution.py
+++ b/solution.py
@@ -118,12 +118,16 @@
 ):
     me = lax.axis_index("tp")
     rows, depth = x_hbm.shape
-    half = rows // 2
+    half = depth // 2
     q_cols = wq_hbm.shape[1]
     k_cols = wk_hbm.shape[1]
     sib, nx, ny = flipped(me, 1), flipped(me, 2), flipped(me, 4)
-    x_copy = pltpu.make_async_copy(x_hbm, held.at[0], x_sem)
-    x_copy.start()
+    x_copies = [
+        pltpu.make_async_copy(x_hbm.at[:, pl.ds(h * half, half)], held.at[0, h], x_sem.at[h])
+        for h in range(2)
+    ]
+    for copy in x_copies:
+        copy.start()
     w_copies = []
     for e in range(8):
         chunk = pl.ds(pl.multiple_of(flipped(me, e) * depth, depth), depth)
@@ -144,11 +148,12 @@
         for copy in copies:
             copy.start()
     greet("tp", (sib, nx, ny))
-    x_copy.wait()
+    for copy in x_copies:
+        copy.wait()
     make, used = sender("tp", send_sems, recv_sems)
 
     def part(slot, h):
-        return held.at[slot, pl.ds(h * half, half), :]
+        return held.at[slot, h]
 
     dx = [make(part(0, h), part(2, h), nx) for h in range(2)]
     dy = [make(part(0, h), part(4, h), ny) for h in range(2)]
@@ -167,55 +172,73 @@
     squares[...] = jnp.zeros_like(squares)
     acc[...] = jnp.zeros_like(acc)
     for e in range(8):
-        gains[e] = gain_ref[pl.ds(flipped(me, e), 1), :]
-
-    def process(e):
-        for copy in w_copies[e]:
-            copy.wait()
-
+        at = pl.ds(pl.multiple_of(flipped(me, e) * depth, depth), depth)
+        gains[e] = gain_ref[:, at]
+
+    def process(e, h):
         @pl.loop(0, rows // 64)
         def _(i):
             at = pl.ds(pl.multiple_of(i * 64, 64), 64)
-            wide = held[e, at, :].astype(jnp.float32)
+            wide = held[e, h, at, :].astype(jnp.float32)
             squares[at, :] += jnp.sum(wide * wide, axis=1, keepdims=True)
-            scaled[at, :] = (wide * gains[e]).astype(jnp.bfloat16)
+            gain = gains[e, :, h * half : (h + 1) * half]
+            scaled[at, :] = (wide * gain).astype(jnp.bfloat16)
 
         @pl.loop(0, (q_cols + 2 * k_cols) // 256)
         def _(t):
             at = pl.ds(pl.multiple_of(t * 256, 256), 256)
             acc[:, at] += jnp.dot(
-                scaled[...], weights[e, :, at], preferred_element_type=jnp.float32
+                scaled[...],
+                weights[e, h * half : (h + 1) * half, at],
+                preferred_element_type=jnp.float32,
             )
 
-    process(0)
+    def weights_of(*slots):
+        for e in slots:
+            for copy in w_copies[e]:
+                copy.wait()
+
+    weights_of(0)
+    process(0, 0)
+    process(0, 1)
+    weights_of(1)
     d1.wait_recv()
-    process(1)
+    process(1, 0)
+    process(1, 1)
     dx[0].wait_recv()
     forward_y.start()
     d3[0].start()
     dy[1].wait_recv()
     forward_x.start()
     d5[1].start()
+    weights_of(2, 3, 4, 5)
+    process(2, 0)
+    process(4, 1)
+    d3[0].wait_recv()
+    process(3, 0)
+    d5[1].wait_recv()
+    process(5, 1)
     dx[1].wait_recv()
     d3[1].start()
     dy[0].wait_recv()
     d5[0].start()
-    process(2)
-    process(4)
-    d3[0].wait_recv()
+    process(2, 1)
+    process(4, 0)
     d3[1].wait_recv()
-    process(3)
+    process(3, 1)
     d5[0].wait_recv()
-    d5[1].wait_recv()
-    process(5)
+    process(5, 0)
+    weights_of(6, 7)
     forward_y.wait_recv()
     d7[0].start()
     forward_x.wait_recv()
     d7[1].start()
-    process(6)
+    process(6, 0)
+    process(6, 1)
     d7[0].wait_recv()
+    process(7, 0)
     d7[1].wait_recv()
-    process(7)
+    process(7, 1)
 
     score_scale = LOG2E / math.sqrt(HEAD_DIM)
     features = depth * 8
@@ -319,7 +342,7 @@
                 )
             return inner
 
-        lax.fori_loop(0, heads, one_head, 0)
+        lax.fori_loop(0, heads, one_head, 0, unroll=2)
         return carried
 
     lax.fori_loop(0, n_cp, visit, 0)
@@ -464,13 +487,13 @@
             in_specs=[any_spec, vmem, any_spec, any_spec, any_spec, vmem, vmem],
             out_specs=(vmem, vmem),
             scratch_shapes=[
-                pltpu.VMEM((8, rows, depth), bf16),
+                pltpu.VMEM((8, 2, rows, depth // 2), bf16),
                 pltpu.VMEM((8, depth, q_cols + 2 * k_cols), bf16),
                 pltpu.VMEM((8, 1, depth), f32),
                 pltpu.VMEM((rows, q_cols + 2 * k_cols), f32),
-                pltpu.VMEM((rows, depth), bf16),
+                pltpu.VMEM((rows, depth // 2), bf16),
                 pltpu.VMEM((rows, 1), f32),
-                dma,
+                dma((2,)),
                 dma((8, 3)),
                 dma((13,)),
                 dma((13,)),
@@ -480,7 +503,7 @@
             ),
             name="project",
         )(
-            checkpoint, norm_gain.reshape(-1, depth), query_weight, key_weight, value_weight, cosine, sine
+            checkpoint, norm_gain.reshape(1, -1), query_weight, key_weight, value_weight, cosine, sine
         )
     else:
         queries, key_value = project_any(

time: 149 us -> 141 us (0.946)
  Pallas kernels: 141 us -> 135 us
    pallas_call x1, Pallas kernels: 37.3 us -> 30.6 us  [shards(): pl.pallas_call(functools.partial(attend_kernel, n_cp), out_shape=(jax.Sha...]
where the time goes in v2:
time: 141 us
  Pallas kernels  135 us (96%)
  local copies, waits for them, and re-layouts  2.88 us (2%)
  other arithmetic  2.62 us (2%)
    pallas_call x1, Pallas kernels, shards(): pl.pallas_call(project_kernel, out_shape=(jax.ShapeDtypeStruct((rows, q_c...  58.9 us
    pallas_call x1, Pallas kernels, shards(): pl.pallas_call(output_kernel, out_shape=jax.ShapeDtypeStruct((rows, out_c...  45.4 us
    pallas_call x1, Pallas kernels, shards(): pl.pallas_call(functools.partial(attend_kernel, n_cp), out_shape=(jax.Sha...  30.6 us
    unnamed x5, local copies, waits for them, and re-layouts  2.88 us

profile of v2, /device:TPU:0, one launch (start us, length us, event | category | flops | bytes accessed | tf_op | source)
XLA Modules:
  0.0 141.1 jit_solution(5110973949482261553)
XLA Ops:
  0.6 0.7 dynamic-slice_multiply_fusion
  1.4 0.1 convert_bitcast_fusion
  1.5 1.8 %fusion = (f32[512,128]{1,0:T(8,128)}, f32[512,128]{1,0:T(8,128)}) fusion(f32[128]{0:T(128)S(1)} %get-tuple-element.12, f32[128]{0:T(128)S(1)} %get-tuple-element.13, f32[512]{0:T(512)S(1)} %bitcast.5), kind=kLoop, calls=%fused_computation.2 | loop fusion | flops 131072 | bytes 527360 | tf_op jit(solution)/shard_map/mul | solution.py:472
  3.3 58.9 %project.1 = (bf16[512,1024]{1,0:T(8,128)(2,1)}, bf16[512,256]{1,0:T(8,128)(2,1)}) custom-call(bf16[512,1024]{1,0:T(8,128)(2,1)} %x_hbm.1, f32[1,8192]{1,0:T(1,128)} %bitcast.4, bf16[8192,1024]{1,0:T(8,128)(2,1)} %wq_hbm.1, bf16[8192,128]{1,0:T(8,128)(2,1)} %wk_hbm.1, bf16[8192,128]{1,0:T(8,128)(2,1)} %wv_hbm.1, f32[512,128]{1,0:T(8,128)} %get-tuple-element.11.cos_ref, ...), custom_call_target="tpu_custom_call" | custom-call | tf_op jit(solution)/shard_map/project/pallas_call | solution.py:481
  62.2 30.6 %attend.1 = (bf16[512,1024]{1,0:T(8,128)(2,1)}, f32[8,512]{1,0:T(8,128)}) custom-call(s32[8]{0:T(128)} %order_ref.1, bf16[512,1024]{1,0:T(8,128)(2,1)} %get-tuple-element.6.q_ref, bf16[512,256]{1,0:T(8,128)(2,1)} %get-tuple-element.7.kv_hbm), custom_call_target="tpu_custom_call" | custom-call | tf_op jit(solution)/shard_map/attend/pallas_call | solution.py:513
  92.8 0.0 copy-start
  92.8 45.4 %project_out.1 = bf16[512,1024]{1,0:T(8,128)(2,1)} custom-call(bf16[512,1024]{1,0:T(8,128)(2,1)} %get-tuple-element.8.a_ref, bf16[1024,8192]{1,0:T(8,128)(2,1)} %w_hbm.1), custom_call_target="tpu_custom_call" | custom-call | tf_op jit(solution)/shard_map/project_out/pallas_call | solution.py:547
  138.2 2.3 %copy.12 = bf16[512,1024]{1,0:T(8,128)(2,1)} copy(bf16[512,1024]{1,0:T(8,128)(2,1)} %project_out.1) | data formatting | bytes 2097152
  140.5 0.0 copy-done
  140.5 0.6 copy.13
  (2 shorter events, 0.0 us)
Async XLA Ops:
  92.8 47.7 %copy-start = (f32[8,512]{1,0:T(8,128)S(1)}, f32[8,512]{1,0:T(8,128)}, u32[]{:S(2)}) copy-start(f32[8,512]{1,0:T(8,128)} %get-tuple-element.17) | copy-start | bytes 49156
